TPU v7x, 16 devices: a 4x2x1 block of a 4x4x8 slice. The times are simulated.
16 devices in a mesh: rep: 4 (over y, z, core), dp: 4 (over x).
Axes of the slice: x: 4, y: 2, z: 1, core: 2. Of those that a mesh axis runs over, the one named last changes fastest.
The devices are a block of a 4x4x8 slice.
Arguments:
- a: bfloat16 [16, 4, 4096, 896], P(('rep', 'dp')), parts along dimension 0
- g: bfloat16 [16, 4, 4096, 2304], P(('rep', 'dp')), parts along dimension 0
Outputs:
- output: bfloat16 [16, 896, 2304], P('rep'), parts along dimension 0
There are 4 independent parts. A program takes and returns all parts, laid end to end along the dimension named above; each array names one.
All inputs are finite; a program needn't handle non-finite values.
Results may differ from a plain program's by a relative error of at most 0.012.
Values are sent between devices in bfloat16 or wider.
A program may use at most 768 MiB of HBM per device.

v0:
```python
import jax
import jax.numpy as jnp


def solution(mesh):
    groups = mesh.shape["rep"]

    def step(a, g):
        a, g = (t.reshape(groups, -1, *t.shape[1:]) for t in (a, g))
        sums = jnp.einsum("rsntd,rsntf->rndf", a, g, preferred_element_type=jnp.float32)
        return sums.astype(jnp.bfloat16).reshape(-1, *sums.shape[2:])

    return step
```

profile of v0, /device:TPU:112, one launch (start us, length us, event | category | flops | bytes accessed | tf_op | source)
XLA Modules:
  0.0 639.9 jit_solution(3067141250328103485)
XLA Ops:
  0.0 78.6 %fusion.3 = f32[1,4,896,2304]{3,2,1,0:T(8,128)} fusion(bf16[1,4,4096,2304]{3,2,1,0:T(8,128)(2,1)} %param.1, bf16[1,4,4096,896]{3,2,1,0:T(8,128)(2,1)} %param), kind=kOutput, calls=%fused_computation.3 | convolution fusion | flops 67645734912 | bytes 137887744 | tf_op jit(solution)/rsntd,rsntf->rndf/dot_general | solution.py:10
  78.6 561.2 %all-reduce.2 = bf16[1,4,896,2304]{3,2,1,0:T(8,128)(2,1)} all-reduce(f32[1,4,896,2304]{3,2,1,0:T(8,128)} %fusion.3), channel_id=1, replica_groups=[4,4]<=[16], use_global_device_ids=true, to_apply=%add.clone | all-reduce | flops 8257536 | bytes 49545216 | tf_op jit(solution)/rsntd,rsntf->rndf/dot_general | solution.py:10
where the time goes:
time: 640 us
  blocking collectives  561 us (88%)
  matrix products  78.6 us (12%)
    dot_general x1, blocking collectives, step(): jnp.einsum('rsntd,rsntf->rndf', a, g, preferred_element_type=jnp.float32)  561 us
    dot_general x1, matrix products, step(): jnp.einsum('rsntd,rsntf->rndf', a, g, preferred_element_type=jnp.float32)  78.6 us

commit v1 on v0

v1 whole, which is shorter than its diff:
```python
import jax
import jax.numpy as jnp
from jax import lax
from jax.sharding import PartitionSpec as P


def solution(mesh):
    def local(a, g):
        outs = []
        for n in range(a.shape[1]):
            part = lax.dot_general(
                a[0, n], g[0, n], (((0,), (0,)), ((), ())), preferred_element_type=jnp.float32
            ).astype(jnp.bfloat16)
            if outs:
                part, outs[-1] = lax.optimization_barrier((part, outs[-1]))
            outs.append(lax.psum(part, "dp"))
        return jnp.stack(outs)

    return jax.shard_map(
        local,
        mesh=mesh,
        in_specs=(P(("rep", "dp")), P(("rep", "dp"))),
        out_specs=P("rep"),
        check_vma=False,
    )
```

time: 640 us -> 394 us (0.62)
  blocking collectives: 561 us -> 0 us
  waiting for transfers between devices: 0 us -> 270 us
  matrix products: 78.6 us -> 96.1 us
  other arithmetic: 0 us -> 13.8 us
  between operations: 0.01 us -> 13.2 us
    dot_general x1 -> x0, blocking collectives: 561 us -> none  [step(): jnp.einsum('rsntd,rsntf->rndf', a, g, preferred_element_type=jnp.float32)]
    psum x0 -> x4, waiting for transfers between devices: none -> 270 us  [local(): outs.append(lax.psum(part, 'dp'))]
    dot_general x1 -> x4, matrix products: 78.6 us -> 96.1 us  [local(): lax.dot_general(a[0, n], g[0, n], (((0,), (0,)), ((), ())), preferred_ele...]
    another operation x0 -> x1, other arithmetic: none -> 13.8 us  [local(): return jnp.stack(outs)]
  transfers between devices with their start and end apart: 0 -> 4, of which waited for: 0 -> 4; matrix products, arithmetic and copies ran while one was open for 0% -> 18% of each run, Pallas kernels for 0% -> 0%
where the time goes in v1:
time: 394 us
  waiting for transfers between devices  270 us (69%)
  matrix products  96.1 us (24%)
  other arithmetic  13.8 us (4%)
  between operations  13.2 us (3%)
    psum x4, waiting for transfers between devices, local(): outs.append(lax.psum(part, 'dp'))  270 us
    dot_general x4, matrix products, local(): lax.dot_general(a[0, n], g[0, n], (((0,), (0,)), ((), ())), preferred_ele...  96.1 us
    another operation x1, other arithmetic, local(): return jnp.stack(outs)  13.8 us
  transfers between devices with their start and end apart: 4, of which 4 were waited for; matrix products, arithmetic and copies ran while one was open for 18% of the time, Pallas kernels for 0%

profile of v1, /device:TPU:112, one launch (start us, length us, event | category | flops | bytes accessed | tf_op | source)
XLA Modules:
  0.0 393.8 jit_solution(12352573572466301977)
XLA Ops:
  6.5 0.0 all-reduce.5.cloned.1.call-start
  6.6 23.9 %fusion.25 = bf16[896,2304]{1,0:T(8,128)(2,1)} fusion(bf16[1,4,4096,2304]{3,2,1,0:T(8,128)(2,1)} %param.3, bf16[1,4,4096,896]{3,2,1,0:T(8,128)(2,1)} %param.2), kind=kOutput, calls=%fused_computation.22 | convolution fusion | flops 16913498112 | bytes 30343168 | tf_op jit(solution)/shard_map/dot_general | solution.py:11
  30.5 0.1 all-reduce.5.cloned.1.call-update
  30.6 0.1 all-reduce.7.cloned.1.call-start
  30.6 24.0 %fusion.20 = bf16[896,2304]{1,0:T(8,128)(2,1)} fusion(bf16[1,4,4096,2304]{3,2,1,0:T(8,128)(2,1)} %param.3, bf16[1,4,4096,896]{3,2,1,0:T(8,128)(2,1)} %param.2), kind=kOutput, calls=%fused_computation.21 | convolution fusion | flops 16913498112 | bytes 30343168 | tf_op jit(solution)/shard_map/dot_general | solution.py:11
  54.6 62.3 %all-reduce.5.cloned.1.call-done = bf16[896,2304]{1,0:T(8,128)(2,1)} async-done(((bf16[896,2304]{1,0:T(8,128)(2,1)}), bf16[896,2304]{1,0:T(8,128)(2,1)}) %all-reduce.5.cloned.1.call-update) | async-done | bytes 4128784 | tf_op jit(solution)/shard_map/psum | solution.py:16
  116.9 0.1 all-reduce.7.cloned.1.call-update
  116.9 0.2 all-reduce.9.cloned.1.call-start
  117.2 24.0 %fusion.30 = bf16[896,2304]{1,0:T(8,128)(2,1)} fusion(bf16[1,4,4096,2304]{3,2,1,0:T(8,128)(2,1)} %param.3, bf16[1,4,4096,896]{3,2,1,0:T(8,128)(2,1)} %param.2), kind=kOutput, calls=%fused_computation.23 | convolution fusion | flops 16913498112 | bytes 30343168 | tf_op jit(solution)/shard_map/dot_general | solution.py:11
  141.2 61.3 %all-reduce.7.cloned.1.call-done = bf16[896,2304]{1,0:T(8,128)(2,1)} async-done(((bf16[896,2304]{1,0:T(8,128)(2,1)}), bf16[896,2304]{1,0:T(8,128)(2,1)}) %all-reduce.7.cloned.1.call-update) | async-done | bytes 4128784 | tf_op jit(solution)/shard_map/psum | solution.py:16
  202.5 0.1 all-reduce.9.cloned.1.call-update
  202.5 0.1 all-reduce.11.cloned.1.call-start
  202.6 24.2 %fusion.35 = bf16[896,2304]{1,0:T(8,128)(2,1)} fusion(bf16[1,4,4096,2304]{3,2,1,0:T(8,128)(2,1)} %param.3, bf16[1,4,4096,896]{3,2,1,0:T(8,128)(2,1)} %param.2), kind=kOutput, calls=%fused_computation.24 | convolution fusion | flops 16913498112 | bytes 30343168 | tf_op jit(solution)/shard_map/dot_general | solution.py:11
  226.8 61.3 %all-reduce.9.cloned.1.call-done = bf16[896,2304]{1,0:T(8,128)(2,1)} async-done(((bf16[896,2304]{1,0:T(8,128)(2,1)}), bf16[896,2304]{1,0:T(8,128)(2,1)}) %all-reduce.9.cloned.1.call-update) | async-done | bytes 4128784 | tf_op jit(solution)/shard_map/psum | solution.py:16
  288.1 0.1 all-reduce.11.cloned.1.call-update
  288.1 85.4 %all-reduce.11.cloned.1.call-done = bf16[1,896,2304]{2,1,0:T(8,128)(2,1)} async-done(((bf16[1,896,2304]{2,1,0:T(8,128)(2,1)}), bf16[1,896,2304]{2,1,0:T(8,128)(2,1)}) %all-reduce.11.cloned.1.call-update) | async-done | bytes 4128784 | tf_op jit(solution)/shard_map/psum | solution.py:16
  373.5 13.8 %pad_maximum_fusion = bf16[4,896,2304]{2,1,0:T(8,128)(2,1)} fusion(bf16[1,896,2304]{2,1,0:T(8,128)(2,1)} %all-reduce.11.cloned.1.call-done, bf16[1,896,2304]{2,1,0:T(8,128)(2,1)} %bitcast.47, bf16[1,896,2304]{2,1,0:T(8,128)(2,1)} %bitcast.46, bf16[1,896,2304]{2,1,0:T(8,128)(2,1)} %bitcast.45), kind=kLoop, calls=%fused_computation.12 | loop fusion | flops 24772608 | bytes 33030144 | tf_op jit(solution)/shard_map/stack | solution.py:17
Async XLA Ops:
  6.5 110.3 %all-reduce.5.cloned.1.call-start = ((), (), s32[]{:S(2)}) async-start(), calls=%async_computation | async-start | bytes 8257536 | tf_op jit(solution)/shard_map/psum | solution.py:16
  30.6 171.9 %all-reduce.7.cloned.1.call-start = ((), (), s32[]{:S(2)}) async-start(), calls=%async_computation.1 | async-start | bytes 8257536 | tf_op jit(solution)/shard_map/psum | solution.py:16
  116.9 171.1 %all-reduce.9.cloned.1.call-start = ((), (), s32[]{:S(2)}) async-start(), calls=%async_computation.2 | async-start | bytes 8257536 | tf_op jit(solution)/shard_map/psum | solution.py:16
  202.5 171.0 %all-reduce.11.cloned.1.call-start = ((), (), s32[]{:S(2)}) async-start(), calls=%async_computation.3 | async-start | bytes 8257536 | tf_op jit(solution)/shard_map/psum | solution.py:16
Sparse Core Ops, SparseCore 0:
  30.7 86.1 all-reduce.4
  119.3 83.1 all-reduce.6
  204.9 83.1 all-reduce.8
  290.3 83.1 all-reduce.10

commit v2 on v1

v2 whole, which is shorter than its diff:
```python
import functools

import jax
import jax.numpy as jnp
from jax import lax
from jax.experimental import pallas as pl
from jax.experimental.pallas import tpu as pltpu
from jax.sharding import PartitionSpec as P

MESH = pl.DeviceIdType.MESH
WIDTH = 256
LAG = 8
FWD = 3
ACC = 4
SEND = 4


def kernel(per, pieces, a_ref, g_ref, o_ref, a_buf, g_buf, acc, sb1, sb2, r1, r2, fin,
           a_sem, g_sem, s1s, s1r, s2s, s2r, ags, agr, fws, fwr, los):
    n = 4
    me = lax.axis_index("dp")
    right, left, opp = lax.rem(me + 1, n), lax.rem(me + 3, n), lax.rem(me + 2, n)
    sides = (right, left)
    rows = fin.shape[1]
    half = rows // 2

    def rows_of(owner, h=None):
        start = owner * rows + (0 if h is None else h * half)
        return pl.ds(pl.multiple_of(start, 16), rows if h is None else half)

    def cols(q):
        return pl.ds(pl.multiple_of(q * WIDTH, WIDTH), WIDTH)

    def split(p):
        return lax.div(p, per), lax.rem(p, per)

    def load_a(m):
        return pltpu.make_async_copy(a_ref.at[0, m], a_buf.at[lax.rem(m, 2)], a_sem.at[lax.rem(m, 2)])

    def load_g(p):
        m, q = split(p)
        slot = lax.rem(p, 3)
        return pltpu.make_async_copy(g_ref.at[0, m, :, cols(q)], g_buf.at[slot], g_sem.at[slot])

    def remote(src, dst, ss, rs, d):
        return pltpu.make_async_remote_copy(
            src_ref=src, dst_ref=dst, send_sem=ss, recv_sem=rs, device_id={"dp": sides[d]}, device_id_type=MESH
        )

    def send1(p, d):
        slot = lax.rem(p, SEND)
        return remote(sb1.at[slot, d], r1.at[p, d], s1s.at[slot, d], s1r.at[p, d], d)

    def send2(p, d):
        slot = lax.rem(p, SEND)
        return remote(sb2.at[slot, d], r2.at[p, d], s2s.at[slot, d], s2r.at[p, d], d)

    def out(p, owner, h=None):
        m, q = split(p)
        return o_ref.at[m, rows_of(owner, h), cols(q)]

    def gather(p, d):
        return remote(fin.at[p], out(p, me), ags.at[p, d], agr.at[p, d], d)

    def forward(p, d):
        block = out(p, (left, right)[d], d)
        return remote(block, block, fws.at[p, d], fwr.at[p, d], d)

    def local(p):
        return pltpu.make_async_copy(fin.at[p], out(p, me), los.at[p])

    load_a(0).start()
    load_g(0).start()
    load_g(1).start()

    barrier = pltpu.get_barrier_semaphore()
    for d in sides:
        pl.semaphore_signal(barrier, inc=1, device_id={"dp": d}, device_id_type=MESH)

    def step(i, carry):
        @pl.when(i < pieces)
        def _():
            m, q = split(i)
            slot, mine = lax.rem(i, SEND), lax.rem(i, ACC)

            @pl.when(q == 0)
            def _():
                load_a(m).wait()

                @pl.when(i + per < pieces)
                def _():
                    load_a(m + 1).start()

            load_g(i).wait()

            @pl.when(i + 2 < pieces)
            def _():
                load_g(i + 2).start()

            acc[mine] = lax.dot_general(
                a_buf[lax.rem(m, 2)], g_buf[lax.rem(i, 3)], (((0,), (0,)), ((), ())),
                preferred_element_type=jnp.float32,
            )

            @pl.when(i == 0)
            def _():
                pl.semaphore_wait(barrier, 2)

            @pl.when(i >= SEND)
            def _():
                for d in range(2):
                    send1(i - SEND, d).wait_send()

            for d in range(2):
                sb1[slot, d, :half] = acc[mine, rows_of(opp, d)].astype(jnp.bfloat16)
                sb1[slot, d, half:] = acc[mine, rows_of(sides[d], 1 - d)].astype(jnp.bfloat16)
            for d in range(2):
                send1(i, d).start()

        @pl.when((i >= 1) & (i < pieces + 1))
        def _():
            p = i - 1
            slot, mine = lax.rem(p, SEND), lax.rem(p, ACC)

            @pl.when(p >= SEND)
            def _():
                for d in range(2):
                    send2(p - SEND, d).wait_send()

            for d in range(2):
                send1(p, d).wait_recv()
                sb2[slot, d] = (
                    acc[mine, rows_of(sides[d], d)] + r1[p, d, :half].astype(jnp.float32)
                ).astype(jnp.bfloat16)
                send2(p, d).start()

        @pl.when((i >= 2) & (i < pieces + 2))
        def _():
            p = i - 2
            mine = lax.rem(p, ACC)
            for d in range(2):
                send2(p, d).wait_recv()
                fin[p, d * half:(d + 1) * half] = (
                    acc[mine, rows_of(me, d)]
                    + r2[p, d].astype(jnp.float32)
                    + r1[p, 1 - d, half:].astype(jnp.float32)
                ).astype(jnp.bfloat16)
            local(p).start()

        @pl.when((i >= 2 + LAG) & (i < pieces + 2 + LAG))
        def _():
            for d in range(2):
                gather(i - 2 - LAG, d).start()

        @pl.when(i >= 2 + LAG + FWD)
        def _():
            p = i - 2 - LAG - FWD
            for d in range(2):
                gather(p, d).wait_recv()
                forward(p, d).start()

        return carry

    lax.fori_loop(0, pieces + 2 + LAG + FWD, step, 0)

    def drain(p, carry):
        local(p).wait()
        for d in range(2):
            gather(p, d).wait_send()
            forward(p, d).wait()
        return carry

    lax.fori_loop(0, pieces, drain, 0)
    for p in range(pieces - SEND, pieces):
        for d in range(2):
            send1(p, d).wait_send()
            send2(p, d).wait_send()


def solution(mesh):
    def local(a, g):
        _, count, tokens, d = a.shape
        ff = g.shape[3]
        per = ff // WIDTH
        pieces = count * per
        rows = d // mesh.shape["dp"]
        dma = pltpu.SemaphoreType.DMA
        bf16 = jnp.bfloat16
        return pl.pallas_call(
            functools.partial(kernel, per, pieces),
            out_shape=jax.ShapeDtypeStruct((count, d, ff), bf16),
            in_specs=[pl.BlockSpec(memory_space=pltpu.HBM)] * 2,
            out_specs=pl.BlockSpec(memory_space=pltpu.HBM),
            scratch_shapes=[
                pltpu.VMEM((2, tokens, d), bf16),
                pltpu.VMEM((3, tokens, WIDTH), bf16),
                pltpu.VMEM((ACC, d, WIDTH), jnp.float32),
                pltpu.VMEM((SEND, 2, rows, WIDTH), bf16),
                pltpu.VMEM((SEND, 2, rows // 2, WIDTH), bf16),
                pltpu.VMEM((pieces, 2, rows, WIDTH), bf16),
                pltpu.VMEM((pieces, 2, rows // 2, WIDTH), bf16),
                pltpu.VMEM((pieces, rows, WIDTH), bf16),
                dma((2,)),
                dma((3,)),
                dma((SEND, 2)),
                dma((pieces, 2)),
                dma((SEND, 2)),
                dma((pieces, 2)),
                dma((pieces, 2)),
                dma((pieces, 2)),
                dma((pieces, 2)),
                dma((pieces, 2)),
                dma((pieces,)),
            ],
            compiler_params=pltpu.CompilerParams(
                collective_id=0, has_side_effects=True, vmem_limit_bytes=60 * 1024 * 1024
            ),
            name="sums",
        )(a, g)

    return jax.shard_map(
        local,
        mesh=mesh,
        in_specs=(P(("rep", "dp")), P(("rep", "dp"))),
        out_specs=P("rep"),
        check_vma=False,
    )
```

time: 394 us -> 297 us (0.75)
  Pallas kernels: 0 us -> 283 us
  waiting for transfers between devices: 270 us -> 0 us
  matrix products: 96.1 us -> 0 us
  other arithmetic: 13.8 us -> 0 us
  local copies, waits for them, and re-layouts: 0 us -> 13.6 us
  between operations: 13.2 us -> 0.01 us
    pallas_call x0 -> x1, Pallas kernels: none -> 283 us  [local(): pl.pallas_call(functools.partial(kernel, per, pieces), out_shape=jax.Shap...]
    psum x4 -> x0, waiting for transfers between devices: 270 us -> none  [local(): outs.append(lax.psum(part, 'dp'))]
    dot_general x4 -> x0, matrix products: 96.1 us -> none  [local(): lax.dot_general(a[0, n], g[0, n], (((0,), (0,)), ((), ())), preferred_ele...]
    another operation x1 -> x0, other arithmetic: 13.8 us -> none  [local(): return jnp.stack(outs)]
    unnamed x0 -> x1, local copies, waits for them, and re-layouts: none -> 13.6 us
  transfers between devices with their start and end apart: 4 -> 0, of which waited for: 4 -> 0; matrix products, arithmetic and copies ran while one was open for 18% -> 0% of each run, Pallas kernels for 0% -> 0%
where the time goes in v2:
time: 297 us
  Pallas kernels  283 us (95%)
  local copies, waits for them, and re-layouts  13.6 us (5%)
    pallas_call x1, Pallas kernels, local(): pl.pallas_call(functools.partial(kernel, per, pieces), out_shape=jax.Shap...  283 us
    unnamed x1, local copies, waits for them, and re-layouts  13.6 us

profile of v2, /device:TPU:112, one launch (start us, length us, event | category | flops | bytes accessed | tf_op | source)
XLA Modules:
  0.0 297.1 jit_solution(5948606214007038424)
XLA Ops:
  0.0 283.4 %sums.1 = bf16[4,896,2304]{2,1,0:T(8,128)(2,1)} custom-call(bf16[1,4,4096,896]{3,2,1,0:T(8,128)(2,1)} %a_ref.1, bf16[1,4,4096,2304]{3,2,1,0:T(8,128)(2,1)} %g_ref.1), custom_call_target="tpu_custom_call" | custom-call | tf_op jit(solution)/shard_map/sums/pallas_call | solution.py:189
  283.4 13.6 %copy.4 = bf16[4,896,2304]{2,1,0:T(8,128)(2,1)} copy(bf16[4,896,2304]{2,1,0:T(8,128)(2,1)} %sums.1) | data formatting | bytes 33030144

commit v3 on v1

v3 whole, which is shorter than its diff:
```python
import functools

import jax
import jax.numpy as jnp
from jax import lax
from jax.experimental import pallas as pl
from jax.experimental.pallas import tpu as pltpu
from jax.sharding import PartitionSpec as P

MESH = pl.DeviceIdType.MESH
BF16 = jnp.bfloat16
WIDTH = 256
GROUP = 3
FIRST = 4
T1, T2, T3, T4 = 2, 3, 5, 6
EVERY, OFFSET = 4, 8
FWD = 3
ACC, V1, V2, SEND = T4 + 1, T4 - T1 + 1, T4 - T3 + 1, 4


def sums_kernel(per, pieces, a_ref, g_ref, res, land, h1, h2, a_buf, g_buf, acc, sb1, sb2, v1, v2,
                a_sem, g_sem, f_sem, s1s, s1r, s2s, s2r, l1, l2, ags, agr, fws, fwr, lon, lof):
    n = 4
    me = lax.axis_index("dp")
    right, left, opp = lax.rem(me + 1, n), lax.rem(me + 3, n), lax.rem(me + 2, n)
    sides = (right, left)
    rows = h1.shape[2]
    half = rows // 2
    groups = pieces // GROUP
    chunk = a_buf.shape[1] // FIRST

    def rows_of(owner, h=None):
        start = owner * rows + (0 if h is None else h * half)
        return pl.ds(pl.multiple_of(start, 16), rows if h is None else half)

    def block(ref, p, width, owner, h=None):
        m, q = lax.div(p, per), lax.rem(p, per)
        return ref.at[m, rows_of(owner, h), pl.ds(pl.multiple_of(q * WIDTH, WIDTH), width)]

    def load_a(m):
        return pltpu.make_async_copy(a_ref.at[0, m], a_buf.at[lax.rem(m, 2)], a_sem.at[lax.rem(m, 2)])

    def load_g(p):
        m, q = lax.div(p, per), lax.rem(p, per)
        slot = lax.rem(p, 3)
        cols = pl.ds(pl.multiple_of(q * WIDTH, WIDTH), WIDTH)
        return pltpu.make_async_copy(g_ref.at[0, m, :, cols], g_buf.at[slot], g_sem.at[slot])

    def first(k):
        t = pl.ds(pl.multiple_of(k * chunk, chunk), chunk)
        return (
            pltpu.make_async_copy(g_ref.at[0, 0, t, pl.ds(0, WIDTH)], g_buf.at[0, t], f_sem.at[k, 0]),
            pltpu.make_async_copy(a_ref.at[0, 0, t], a_buf.at[0, t], f_sem.at[k, 1]),
        )

    def remote(src, dst, ss, rs, d):
        return pltpu.make_async_remote_copy(
            src_ref=src, dst_ref=dst, send_sem=ss, recv_sem=rs, device_id={"dp": sides[d]}, device_id_type=MESH
        )

    def send1(p, d):
        slot = lax.rem(p, SEND)
        return remote(sb1.at[slot, d], h1.at[p, d], s1s.at[slot, d], s1r.at[p, d], d)

    def send2(p, d):
        slot = lax.rem(p, SEND)
        return remote(sb2.at[slot, d], h2.at[p, d], s2s.at[slot, d], s2r.at[p, d], d)

    def load1(p, d):
        slot = lax.rem(p, V1)
        return pltpu.make_async_copy(h1.at[p, d], v1.at[slot, d], l1.at[slot, d])

    def load2(p, d):
        slot = lax.rem(p, V2)
        return pltpu.make_async_copy(h2.at[p, d], v2.at[slot, d], l2.at[slot, d])

    def gather(k, d):
        p, width = k * GROUP, GROUP * WIDTH
        return remote(block(res, p, width, me), block(land, p, width, me), ags.at[k, d], agr.at[k, d], d)

    def forward(k, d):
        b = block(land, k * GROUP, GROUP * WIDTH, (left, right)[d], d)
        return remote(b, b, fws.at[k, d], fwr.at[k, d], d)

    def keep_near(k, d):
        p, width, owner = k * GROUP, GROUP * WIDTH, (left, right)[d]
        return pltpu.make_async_copy(block(land, p, width, owner), block(res, p, width, owner), lon.at[k, d])

    def keep_far(k, d):
        p, width = k * GROUP, GROUP * WIDTH
        return pltpu.make_async_copy(block(land, p, width, opp, d), block(res, p, width, opp, d), lof.at[k, d])

    def gather_start(k):
        for d in range(2):
            gather(k, d).start()

    def forward_start(k):
        for d in range(2):
            gather(k, d).wait_recv()
            forward(k, d).start()
            keep_near(k, d).start()

    def far_start(k):
        for d in range(2):
            forward(k, d).wait_recv()
            keep_far(k, d).start()

    for k in range(FIRST):
        for copy in first(k):
            copy.start()
    load_g(1).start()

    barrier = pltpu.get_barrier_semaphore()
    for d in sides:
        pl.semaphore_signal(barrier, inc=1, device_id={"dp": d}, device_id_type=MESH)

    def product(lhs, rhs):
        return lax.dot_general(lhs, rhs, (((0,), (0,)), ((), ())), preferred_element_type=jnp.float32)

    acc[0] = jnp.zeros_like(acc[0])

    def first_step(k, carry):
        for copy in first(k):
            copy.wait()
        t = pl.ds(pl.multiple_of(k * chunk, chunk), chunk)
        acc[0] += product(a_buf[0, t], g_buf[0, t])
        return carry

    lax.fori_loop(0, FIRST, first_step, 0)
    pl.semaphore_wait(barrier, 2)

    def step(i, carry):
        @pl.when(i < pieces)
        def _():
            m, q = lax.div(i, per), lax.rem(i, per)
            slot, mine = lax.rem(i, SEND), lax.rem(i, ACC)

            @pl.when(i + 2 < pieces)
            def _():
                load_g(i + 2).start()

            @pl.when((q == 0) & (i + per < pieces))
            def _():
                load_a(m + 1).start()

            @pl.when(i > 0)
            def _():
                @pl.when(q == 0)
                def _():
                    load_a(m).wait()

                load_g(i).wait()
                acc[mine] = product(a_buf[lax.rem(m, 2)], g_buf[lax.rem(i, 3)])

            @pl.when(i >= SEND)
            def _():
                for d in range(2):
                    send1(i - SEND, d).wait_send()

            for d in range(2):
                sb1[slot, d, :half] = acc[mine, rows_of(opp, d)].astype(BF16)
                sb1[slot, d, half:] = acc[mine, rows_of(sides[d], 1 - d)].astype(BF16)
            for d in range(2):
                send1(i, d).start()

        @pl.when((i >= T1) & (i < pieces + T1))
        def _():
            for d in range(2):
                send1(i - T1, d).wait_recv()
                load1(i - T1, d).start()

        @pl.when((i >= T2) & (i < pieces + T2))
        def _():
            p = i - T2
            slot, mine, here = lax.rem(p, SEND), lax.rem(p, ACC), lax.rem(p, V1)

            @pl.when(p >= SEND)
            def _():
                for d in range(2):
                    send2(p - SEND, d).wait_send()

            for d in range(2):
                load1(p, d).wait()
                sb2[slot, d] = (acc[mine, rows_of(sides[d], d)] + v1[here, d, :half].astype(jnp.float32)).astype(BF16)
            for d in range(2):
                send2(p, d).start()

        @pl.when((i >= T3) & (i < pieces + T3))
        def _():
            for d in range(2):
                send2(i - T3, d).wait_recv()
                load2(i - T3, d).start()

        @pl.when(i >= T4)
        def _():
            p = i - T4
            m, q = lax.div(p, per), lax.rem(p, per)
            mine, one, two = lax.rem(p, ACC), lax.rem(p, V1), lax.rem(p, V2)
            cols = pl.ds(pl.multiple_of(q * WIDTH, WIDTH), WIDTH)
            for d in range(2):
                load2(p, d).wait()
                res[m, rows_of(me, d), cols] = (
                    acc[mine, rows_of(me, d)]
                    + v2[two, d].astype(jnp.float32)
                    + v1[one, 1 - d, half:].astype(jnp.float32)
                ).astype(BF16)

        t = i - OFFSET

        @pl.when((t >= 0) & (lax.rem(t, EVERY) == 0))
        def _():
            gather_start(lax.div(t, EVERY))

        @pl.when((t >= FWD) & (lax.rem(t - FWD, EVERY) == 0))
        def _():
            k = lax.div(t - FWD, EVERY)
            forward_start(k)

            @pl.when(k >= 2)
            def _():
                far_start(k - 2)

        return carry

    last = pieces + T4
    lax.fori_loop(0, last, step, 0)

    def over(f, start, stop):
        def body(k, carry):
            f(k)
            return carry

        lax.fori_loop(start, stop, body, 0)

    gathered = (last - 1 - OFFSET) // EVERY + 1
    forwarded = (last - 1 - OFFSET - FWD) // EVERY + 1
    over(gather_start, gathered, groups)
    over(forward_start, forwarded, groups)
    over(far_start, max(forwarded - 2, 0), groups)

    def drain(k):
        for d in range(2):
            gather(k, d).wait_send()
            forward(k, d).wait_send()
            keep_near(k, d).wait()
            keep_far(k, d).wait()

    for p in range(pieces - SEND, pieces):
        for d in range(2):
            send1(p, d).wait_send()
            send2(p, d).wait_send()
    over(drain, 0, groups)


def write_kernel(res, o_ref, sem):
    count = res.shape[0]
    copies = [pltpu.make_async_copy(res.at[m], o_ref.at[m], sem.at[m]) for m in range(count)]
    for copy in copies:
        copy.start()
    for copy in copies:
        copy.wait()


def solution(mesh):
    def local(a, g):
        _, count, tokens, d = a.shape
        ff = g.shape[3]
        per = ff // WIDTH
        pieces = count * per
        groups = pieces // GROUP
        rows = d // mesh.shape["dp"]
        dma = pltpu.SemaphoreType.DMA
        hbm = pl.BlockSpec(memory_space=pltpu.HBM)
        res = pl.pallas_call(
            functools.partial(sums_kernel, per, pieces),
            out_shape=(
                pltpu.VMEM((count, d, ff), BF16),
                jax.ShapeDtypeStruct((count, d, ff), BF16),
                jax.ShapeDtypeStruct((pieces, 2, rows, WIDTH), BF16),
                jax.ShapeDtypeStruct((pieces, 2, rows // 2, WIDTH), BF16),
            ),
            in_specs=[hbm] * 2,
            out_specs=(pl.BlockSpec(memory_space=pltpu.VMEM), hbm, hbm, hbm),
            scratch_shapes=[
                pltpu.VMEM((2, tokens, d), BF16),
                pltpu.VMEM((3, tokens, WIDTH), BF16),
                pltpu.VMEM((ACC, d, WIDTH), jnp.float32),
                pltpu.VMEM((SEND, 2, rows, WIDTH), BF16),
                pltpu.VMEM((SEND, 2, rows // 2, WIDTH), BF16),
                pltpu.VMEM((V1, 2, rows, WIDTH), BF16),
                pltpu.VMEM((V2, 2, rows // 2, WIDTH), BF16),
                dma((2,)),
                dma((3,)),
                dma((FIRST, 2)),
                dma((SEND, 2)),
                dma((pieces, 2)),
                dma((SEND, 2)),
                dma((pieces, 2)),
                dma((V1, 2)),
                dma((V2, 2)),
                dma((groups, 2)),
                dma((groups, 2)),
                dma((groups, 2)),
                dma((groups, 2)),
                dma((groups, 2)),
                dma((groups, 2)),
            ],
            compiler_params=pltpu.CompilerParams(
                collective_id=0, has_side_effects=True, vmem_limit_bytes=40 * 1024 * 1024
            ),
            name="sums",
        )(a, g)[0]
        return pl.pallas_call(
            write_kernel,
            out_shape=jax.ShapeDtypeStruct((count, d, ff), BF16),
            in_specs=[pl.BlockSpec(memory_space=pltpu.VMEM)],
            out_specs=hbm,
            scratch_shapes=[dma((count,))],
            compiler_params=pltpu.CompilerParams(vmem_limit_bytes=4 * 1024 * 1024),
            name="write",
        )(res)

    return jax.shard_map(
        local,
        mesh=mesh,
        in_specs=(P(("rep", "dp")), P(("rep", "dp"))),
        out_specs=P("rep"),
        check_vma=False,
    )
```

time: 394 us -> 285 us (0.72)
  Pallas kernels: 0 us -> 285 us
  waiting for transfers between devices: 270 us -> 0 us
  matrix products: 96.1 us -> 0 us
  other arithmetic: 13.8 us -> 0 us
  between operations: 13.2 us -> 0.01 us
    pallas_call x0 -> x2, Pallas kernels: none -> 285 us  [the longest x1 279 us: local(): pl.pallas_call(functools.partial(sums_kernel, per, pieces), out_shape=(pl...]
    psum x4 -> x0, waiting for transfers between devices: 270 us -> none  [local(): outs.append(lax.psum(part, 'dp'))]
    dot_general x4 -> x0, matrix products: 96.1 us -> none  [local(): lax.dot_general(a[0, n], g[0, n], (((0,), (0,)), ((), ())), preferred_ele...]
    another operation x1 -> x0, other arithmetic: 13.8 us -> none  [local(): return jnp.stack(outs)]
  transfers between devices with their start and end apart: 4 -> 0, of which waited for: 4 -> 0; matrix products, arithmetic and copies ran while one was open for 18% -> 0% of each run, Pallas kernels for 0% -> 0%
where the time goes in v3:
time: 285 us
  Pallas kernels  285 us (100%)
    pallas_call x1, Pallas kernels, local(): pl.pallas_call(functools.partial(sums_kernel, per, pieces), out_shape=(pl...  279 us
    pallas_call x1, Pallas kernels, local(): pl.pallas_call(write_kernel, out_shape=jax.ShapeDtypeStruct((count, d, ff...  5.98 us

profile of v3, /device:TPU:112, one launch (start us, length us, event | category | flops | bytes accessed | tf_op | source)
XLA Modules:
  0.0 284.8 jit_solution(7979785004186333140)
XLA Ops:
  0.0 278.8 %sums.1 = (bf16[4,896,2304]{2,1,0:T(8,128)(2,1)S(1)}, bf16[4,896,2304]{2,1,0:T(8,128)(2,1)}, bf16[36,2,224,256]{3,2,1,0:T(8,128)(2,1)}, bf16[36,2,112,256]{3,2,1,0:T(8,128)(2,1)}) custom-call(bf16[1,4,4096,896]{3,2,1,0:T(8,128)(2,1)} %a_ref.1, bf16[1,4,4096,2304]{3,2,1,0:T(8,128)(2,1)} %g_ref.1), custom_call_target="tpu_custom_call" | custom-call | tf_op jit(solution)/shard_map/sums/pallas_call | solution.py:274
  278.8 6.0 %write.1 = bf16[4,896,2304]{2,1,0:T(8,128)(2,1)} custom-call(bf16[4,896,2304]{2,1,0:T(8,128)(2,1)S(1)} %get-tuple-element.6.res), custom_call_target="tpu_custom_call" | custom-call | tf_op jit(solution)/shard_map/write/pallas_call | solution.py:313

commit v4 on v3

--- a/solution.py
+++ b/solution.py
@@ -12,10 +12,13 @@
 WIDTH = 256
 GROUP = 3
 FIRST = 4
-T1, T2, T3, T4 = 2, 3, 5, 6
-EVERY, OFFSET = 4, 8
+T1, T2, T3, T4 = 3, 4, 6, 7
+EVERY, OFFSET = 4, 9
+PARTS = 4
 FWD = 3
 ACC, V1, V2, SEND = T4 + 1, T4 - T1 + 1, T4 - T3 + 1, 4
+RECV = 8
+KEEP = 4
 
 
 def sums_kernel(per, pieces, a_ref, g_ref, res, land, h1, h2, a_buf, g_buf, acc, sb1, sb2, v1, v2,
@@ -60,11 +63,11 @@
 
     def send1(p, d):
         slot = lax.rem(p, SEND)
-        return remote(sb1.at[slot, d], h1.at[p, d], s1s.at[slot, d], s1r.at[p, d], d)
+        return remote(sb1.at[slot, d], h1.at[p, d], s1s.at[slot, d], s1r.at[lax.rem(p, RECV), d], d)
 
     def send2(p, d):
         slot = lax.rem(p, SEND)
-        return remote(sb2.at[slot, d], h2.at[p, d], s2s.at[slot, d], s2r.at[p, d], d)
+        return remote(sb2.at[slot, d], h2.at[p, d], s2s.at[slot, d], s2r.at[lax.rem(p, RECV), d], d)
 
     def load1(p, d):
         slot = lax.rem(p, V1)
@@ -75,40 +78,61 @@
         return pltpu.make_async_copy(h2.at[p, d], v2.at[slot, d], l2.at[slot, d])
 
     def gather(k, d):
-        p, width = k * GROUP, GROUP * WIDTH
-        return remote(block(res, p, width, me), block(land, p, width, me), ags.at[k, d], agr.at[k, d], d)
-
-    def forward(k, d):
-        b = block(land, k * GROUP, GROUP * WIDTH, (left, right)[d], d)
-        return remote(b, b, fws.at[k, d], fwr.at[k, d], d)
+        b = block(land, k * GROUP, GROUP * WIDTH, me)
+        return remote(block(res, k * GROUP, GROUP * WIDTH, me), b, ags.at[lax.rem(k, KEEP), d], agr.at[k, d], d)
+
+    def forward(k, d, to):
+        p, width, owner = k * GROUP, GROUP * WIDTH, (left, right)[d]
+        return remote(
+            block(land, p, width, owner, d), block(to, p, width, owner, d), fws.at[lax.rem(k, KEEP), d], fwr.at[k, d], d
+        )
 
     def keep_near(k, d):
         p, width, owner = k * GROUP, GROUP * WIDTH, (left, right)[d]
-        return pltpu.make_async_copy(block(land, p, width, owner), block(res, p, width, owner), lon.at[k, d])
+        return pltpu.make_async_copy(
+            block(land, p, width, owner), block(res, p, width, owner), lon.at[lax.rem(k, KEEP), d]
+        )
 
     def keep_far(k, d):
         p, width = k * GROUP, GROUP * WIDTH
-        return pltpu.make_async_copy(block(land, p, width, opp, d), block(res, p, width, opp, d), lof.at[k, d])
+        return pltpu.make_async_copy(
+            block(land, p, width, opp, d), block(res, p, width, opp, d), lof.at[lax.rem(k, KEEP), d]
+        )
 
     def gather_start(k):
+        @pl.when(k >= KEEP)
+        def _():
+            for d in range(2):
+                gather(k - KEEP, d).wait_send()
+
         for d in range(2):
             gather(k, d).start()
 
-    def forward_start(k):
+    def forward_start(k, to=land):
+        @pl.when(k >= KEEP)
+        def _():
+            for d in range(2):
+                forward(k - KEEP, d, land).wait_send()
+                keep_near(k - KEEP, d).wait()
+
         for d in range(2):
             gather(k, d).wait_recv()
-            forward(k, d).start()
+            forward(k, d, to).start()
             keep_near(k, d).start()
 
     def far_start(k):
-        for d in range(2):
-            forward(k, d).wait_recv()
+        @pl.when(k >= KEEP)
+        def _():
+            for d in range(2):
+                keep_far(k - KEEP, d).wait()
+
+        for d in range(2):
+            forward(k, d, land).wait_recv()
             keep_far(k, d).start()
 
     for k in range(FIRST):
         for copy in first(k):
             copy.start()
-    load_g(1).start()
 
     barrier = pltpu.get_barrier_semaphore()
     for d in sides:
@@ -123,6 +147,11 @@
         for copy in first(k):
             copy.wait()
         t = pl.ds(pl.multiple_of(k * chunk, chunk), chunk)
+
+        @pl.when(k == FIRST - 1)
+        def _():
+            load_g(1).start()
+
         acc[0] += product(a_buf[0, t], g_buf[0, t])
         return carry
 
@@ -234,27 +263,43 @@
 
     gathered = (last - 1 - OFFSET) // EVERY + 1
     forwarded = (last - 1 - OFFSET - FWD) // EVERY + 1
+    final = groups - 1
     over(gather_start, gathered, groups)
-    over(forward_start, forwarded, groups)
-    over(far_start, max(forwarded - 2, 0), groups)
-
-    def drain(k):
-        for d in range(2):
-            gather(k, d).wait_send()
-            forward(k, d).wait_send()
-            keep_near(k, d).wait()
-            keep_far(k, d).wait()
+    over(forward_start, forwarded, final)
+    forward_start(final, res)
+    over(far_start, max(forwarded - 2, 0), final)
 
     for p in range(pieces - SEND, pieces):
         for d in range(2):
             send1(p, d).wait_send()
             send2(p, d).wait_send()
-    over(drain, 0, groups)
+
+    def drain(k):
+        for d in range(2):
+            gather(k, d).wait_send()
+            keep_near(k, d).wait()
+            forward(k, d, land).wait_send()
+
+    def drain_far(k):
+        for d in range(2):
+            keep_far(k, d).wait()
+
+    over(drain, groups - KEEP, groups)
+    over(drain_far, final - KEEP, final)
+    for d in range(2):
+        forward(final, d, res).wait_recv()
 
 
 def write_kernel(res, o_ref, sem):
-    count = res.shape[0]
-    copies = [pltpu.make_async_copy(res.at[m], o_ref.at[m], sem.at[m]) for m in range(count)]
+    count, d, _ = res.shape
+    step = d // PARTS
+    copies = [
+        pltpu.make_async_copy(
+            res.at[m, pl.ds(k * step, step)], o_ref.at[m, pl.ds(k * step, step)], sem.at[m, k]
+        )
+        for m in range(count)
+        for k in range(PARTS)
+    ]
     for copy in copies:
         copy.start()
     for copy in copies:
@@ -293,17 +338,17 @@
                 dma((3,)),
                 dma((FIRST, 2)),
                 dma((SEND, 2)),
-                dma((pieces, 2)),
+                dma((RECV, 2)),
                 dma((SEND, 2)),
-                dma((pieces, 2)),
+                dma((RECV, 2)),
                 dma((V1, 2)),
                 dma((V2, 2)),
+                dma((KEEP, 2)),
                 dma((groups, 2)),
+                dma((KEEP, 2)),
                 dma((groups, 2)),
-                dma((groups, 2)),
-                dma((groups, 2)),
-                dma((groups, 2)),
-                dma((groups, 2)),
+                dma((KEEP, 2)),
+                dma((KEEP, 2)),
             ],
             compiler_params=pltpu.CompilerParams(
                 collective_id=0, has_side_effects=True, vmem_limit_bytes=40 * 1024 * 1024
@@ -315,7 +360,7 @@
             out_shape=jax.ShapeDtypeStruct((count, d, ff), BF16),
             in_specs=[pl.BlockSpec(memory_space=pltpu.VMEM)],
             out_specs=hbm,
-            scratch_shapes=[dma((count,))],
+            scratch_shapes=[dma((count, PARTS))],
             compiler_params=pltpu.CompilerParams(vmem_limit_bytes=4 * 1024 * 1024),
             name="write",
         )(res)

time: 285 us -> 283 us (level)
  no operation moved by 1% of the time
where the time goes in v4:
time: 283 us
  Pallas kernels  283 us (100%)
    pallas_call x1, Pallas kernels, local(): pl.pallas_call(functools.partial(sums_kernel, per, pieces), out_shape=(pl...  277 us
    pallas_call x1, Pallas kernels, local(): pl.pallas_call(write_kernel, out_shape=jax.ShapeDtypeStruct((count, d, ff...  5.9 us

profile of v4, /device:TPU:112, one launch (start us, length us, event | category | flops | bytes accessed | tf_op | source)
XLA Modules:
  0.0 282.7 jit_solution(11079900858917964654)
XLA Ops:
  0.0 276.8 %sums.1 = (bf16[4,896,2304]{2,1,0:T(8,128)(2,1)S(1)}, bf16[4,896,2304]{2,1,0:T(8,128)(2,1)}, bf16[36,2,224,256]{3,2,1,0:T(8,128)(2,1)}, bf16[36,2,112,256]{3,2,1,0:T(8,128)(2,1)}) custom-call(bf16[1,4,4096,896]{3,2,1,0:T(8,128)(2,1)} %a_ref.1, bf16[1,4,4096,2304]{3,2,1,0:T(8,128)(2,1)} %g_ref.1), custom_call_target="tpu_custom_call" | custom-call | tf_op jit(solution)/shard_map/sums/pallas_call | solution.py:319
  276.8 5.9 %write.1 = bf16[4,896,2304]{2,1,0:T(8,128)(2,1)} custom-call(bf16[4,896,2304]{2,1,0:T(8,128)(2,1)S(1)} %get-tuple-element.6.res), custom_call_target="tpu_custom_call" | custom-call | tf_op jit(solution)/shard_map/write/pallas_call | solution.py:358

commit v5 on v4

--- a/solution.py
+++ b/solution.py
@@ -14,11 +14,11 @@
 FIRST = 4
 T1, T2, T3, T4 = 3, 4, 6, 7
 EVERY, OFFSET = 4, 9
-PARTS = 4
+LATER = 2
+DEEP = 3
 FWD = 3
 ACC, V1, V2, SEND = T4 + 1, T4 - T1 + 1, T4 - T3 + 1, 4
-RECV = 8
-KEEP = 4
+RECV, KEEP = 7, 4
 
 
 def sums_kernel(per, pieces, a_ref, g_ref, res, land, h1, h2, a_buf, g_buf, acc, sb1, sb2, v1, v2,
@@ -29,7 +29,8 @@
     sides = (right, left)
     rows = h1.shape[2]
     half = rows // 2
-    groups = pieces // GROUP
+    odd = lax.rem(lax.axis_index("rep"), 2)
+    groups = pieces // GROUP - odd * LATER
     chunk = a_buf.shape[1] // FIRST
 
     def rows_of(owner, h=None):
@@ -71,11 +72,11 @@
 
     def load1(p, d):
         slot = lax.rem(p, V1)
-        return pltpu.make_async_copy(h1.at[p, d], v1.at[slot, d], l1.at[slot, d])
+        return pltpu.make_async_copy(h1.at[p, d], v1.at[slot, d], l1.at[lax.rem(p, 2), d])
 
     def load2(p, d):
         slot = lax.rem(p, V2)
-        return pltpu.make_async_copy(h2.at[p, d], v2.at[slot, d], l2.at[slot, d])
+        return pltpu.make_async_copy(h2.at[p, d], v2.at[slot, d], l2.at[lax.rem(p, 2), d])
 
     def gather(k, d):
         b = block(land, k * GROUP, GROUP * WIDTH, me)
@@ -133,6 +134,7 @@
     for k in range(FIRST):
         for copy in first(k):
             copy.start()
+    load_g(1).start()
 
     barrier = pltpu.get_barrier_semaphore()
     for d in sides:
@@ -147,11 +149,6 @@
         for copy in first(k):
             copy.wait()
         t = pl.ds(pl.multiple_of(k * chunk, chunk), chunk)
-
-        @pl.when(k == FIRST - 1)
-        def _():
-            load_g(1).start()
-
         acc[0] += product(a_buf[0, t], g_buf[0, t])
         return carry
 
@@ -263,11 +260,27 @@
 
     gathered = (last - 1 - OFFSET) // EVERY + 1
     forwarded = (last - 1 - OFFSET - FWD) // EVERY + 1
+    kept = max(forwarded - 2, 0)
     final = groups - 1
-    over(gather_start, gathered, groups)
-    over(forward_start, forwarded, final)
-    forward_start(final, res)
-    over(far_start, max(forwarded - 2, 0), final)
+
+    def tail(t):
+        @pl.when((t >= gathered) & (t < groups))
+        def _():
+            gather_start(t)
+
+        @pl.when((t - DEEP >= forwarded) & (t - DEEP < final))
+        def _():
+            forward_start(t - DEEP)
+
+        @pl.when(t - DEEP == final)
+        def _():
+            forward_start(final, res)
+
+        @pl.when((t - DEEP - 2 >= kept) & (t - DEEP - 2 < final))
+        def _():
+            far_start(t - DEEP - 2)
+
+    over(tail, min(gathered, forwarded + DEEP, kept + DEEP + 2), groups + DEEP + 2)
 
     for p in range(pieces - SEND, pieces):
         for d in range(2):
@@ -290,20 +303,78 @@
         forward(final, d, res).wait_recv()
 
 
-def write_kernel(res, o_ref, sem):
-    count, d, _ = res.shape
-    step = d // PARTS
-    copies = [
-        pltpu.make_async_copy(
-            res.at[m, pl.ds(k * step, step)], o_ref.at[m, pl.ds(k * step, step)], sem.at[m, k]
-        )
-        for m in range(count)
-        for k in range(PARTS)
-    ]
-    for copy in copies:
-        copy.start()
-    for copy in copies:
-        copy.wait()
+def later_kernel(per, groups, res, after, land, sg, rg, sf, rf, sl):
+    n = 4
+    odd = lax.rem(lax.axis_index("rep"), 2)
+    me = lax.axis_index("dp")
+    right, left = lax.rem(me + 1, n), lax.rem(me + 3, n)
+    sides = (right, left)
+    rows = res.shape[1] // n
+    half = rows // 2
+
+    def rows_of(owner, h=0, size=rows):
+        return pl.ds(pl.multiple_of(owner * rows + h * half, 16), size)
+
+    def own(k):
+        p = (groups - LATER + k) * GROUP
+        return res.at[p // per, rows_of(me), pl.ds(p % per * WIDTH, GROUP * WIDTH)]
+
+    def remote(src, dst, ss, rs, d):
+        return pltpu.make_async_remote_copy(
+            src_ref=src, dst_ref=dst, send_sem=ss, recv_sem=rs, device_id={"dp": sides[d]}, device_id_type=MESH
+        )
+
+    def gather(k, d):
+        return remote(own(k), land.at[k, rows_of(me)], sg.at[k, d], rg.at[k, d], d)
+
+    def forward(k, d):
+        b = land.at[k, rows_of((left, right)[d], d, half)]
+        return remote(b, b, sf.at[k, d], rf.at[k, d], d)
+
+    def keep(k):
+        return pltpu.make_async_copy(own(k), land.at[k, rows_of(me)], sl.at[k])
+
+    @pl.when(odd == 1)
+    def _():
+        barrier = pltpu.get_barrier_semaphore()
+        for d in sides:
+            pl.semaphore_signal(barrier, inc=1, device_id={"dp": d}, device_id_type=MESH)
+        pl.semaphore_wait(barrier, 2)
+        every = [(k, d) for k in range(LATER) for d in range(2)]
+        for k, d in every:
+            gather(k, d).start()
+        for k in range(LATER):
+            keep(k).start()
+        for k, d in every:
+            gather(k, d).wait_recv()
+            forward(k, d).start()
+        for k in range(LATER):
+            keep(k).wait()
+        for k, d in every:
+            gather(k, d).wait_send()
+            forward(k, d).wait()
+
+
+def write_kernel(per, begin, end_even, end_odd, res, *rest):
+    o_ref, done, sem = rest[-3:]
+    odd = lax.rem(lax.axis_index("rep"), 2)
+    end = (1 - odd) * end_even + odd * end_odd
+
+    def copy(k):
+        p = k * GROUP
+        to = o_ref.at[p // per, :, pl.ds(p % per * WIDTH, GROUP * WIDTH)]
+        part = res.at[k - begin] if begin else res.at[p // per, :, pl.ds(p % per * WIDTH, GROUP * WIDTH)]
+        return pltpu.make_async_copy(part, to, sem.at[k])
+
+    for k in range(begin, max(end_even, end_odd)):
+        @pl.when(k < end)
+        def _():
+            copy(k).start()
+
+    for k in range(begin, max(end_even, end_odd)):
+        @pl.when(k < end)
+        def _():
+            copy(k).wait()
 
 
 def solution(mesh):
@@ -312,10 +383,12 @@
         ff = g.shape[3]
         per = ff // WIDTH
         pieces = count * per
+        rows = d // mesh.shape["dp"]
         groups = pieces // GROUP
-        rows = d // mesh.shape["dp"]
         dma = pltpu.SemaphoreType.DMA
+        vmem = pl.BlockSpec(memory_space=pltpu.VMEM)
         hbm = pl.BlockSpec(memory_space=pltpu.HBM)
+        token = jax.ShapeDtypeStruct((8, 128), BF16)
         res = pl.pallas_call(
             functools.partial(sums_kernel, per, pieces),
             out_shape=(
@@ -325,7 +398,7 @@
                 jax.ShapeDtypeStruct((pieces, 2, rows // 2, WIDTH), BF16),
             ),
             in_specs=[hbm] * 2,
-            out_specs=(pl.BlockSpec(memory_space=pltpu.VMEM), hbm, hbm, hbm),
+            out_specs=(vmem, hbm, hbm, hbm),
             scratch_shapes=[
                 pltpu.VMEM((2, tokens, d), BF16),
                 pltpu.VMEM((3, tokens, WIDTH), BF16),
@@ -341,8 +414,8 @@
                 dma((RECV, 2)),
                 dma((SEND, 2)),
                 dma((RECV, 2)),
-                dma((V1, 2)),
-                dma((V2, 2)),
+                dma((2, 2)),
+                dma((2, 2)),
                 dma((KEEP, 2)),
                 dma((groups, 2)),
                 dma((KEEP, 2)),
@@ -355,15 +428,33 @@
             ),
             name="sums",
         )(a, g)[0]
-        return pl.pallas_call(
-            write_kernel,
-            out_shape=jax.ShapeDtypeStruct((count, d, ff), BF16),
-            in_specs=[pl.BlockSpec(memory_space=pltpu.VMEM)],
-            out_specs=hbm,
-            scratch_shapes=[dma((count, PARTS))],
-            compiler_params=pltpu.CompilerParams(vmem_limit_bytes=4 * 1024 * 1024),
-            name="write",
-        )(res)
+
+        def write(begin, end_even, end_odd, *args):
+            return pl.pallas_call(
+                functools.partial(write_kernel, per, begin, end_even, end_odd),
+                out_shape=(jax.ShapeDtypeStruct((count, d, ff), BF16), token),
+                in_specs=[vmem, hbm][: len(args)],
+                out_specs=(hbm, hbm),
+                input_output_aliases={1: 0} if begin else {},
+                scratch_shapes=[dma((groups,))],
+                compiler_params=pltpu.CompilerParams(vmem_limit_bytes=4 * 1024 * 1024),
+                name=f"write{begin}",
+            )(*args)
+
+        split = groups - LATER
+        out, done = write(0, groups, split, res)
+        later = pl.pallas_call(
+            functools.partial(later_kernel, per, groups),
+            out_shape=pltpu.VMEM((LATER, d, GROUP * WIDTH), BF16),
+            in_specs=[vmem, hbm],
+            out_specs=vmem,
+            scratch_shapes=[dma((LATER, 2))] * 4 + [dma((LATER,))],
+            compiler_params=pltpu.CompilerParams(
+                collective_id=1, has_side_effects=True, vmem_limit_bytes=4 * 1024 * 1024
+            ),
+            name="later",
+        )(res, done)
+        return write(split, split, groups, later, out)[0]
 
     return jax.shard_map(
         local,

time: 283 us -> 277 us (0.979); the launches traced: 283 us -> 274 us
  Pallas kernels: 283 us -> 274 us
    pallas_call x1, Pallas kernels: 277 us -> 267 us  [local(): pl.pallas_call(functools.partial(sums_kernel, per, pieces), out_shape=(pl...]
    pallas_call x1 -> x3, Pallas kernels: 5.9 us -> 6.23 us  [the longest x2 6.04 us: write(): pl.pallas_call(functools.partial(write_kernel, per, begin, end_even, end_...]
where the time goes in v5:
time: 277 us; the launch traced here: 274 us
  Pallas kernels  274 us (99%)
    pallas_call x1, Pallas kernels, local(): pl.pallas_call(functools.partial(sums_kernel, per, pieces), out_shape=(pl...  267 us
    pallas_call x2, Pallas kernels, write(): pl.pallas_call(functools.partial(write_kernel, per, begin, end_even, end_...  6.04 us

profile of v5, /device:TPU:112, one launch (start us, length us, event | category | flops | bytes accessed | tf_op | source)
XLA Modules:
  0.0 273.6 jit_solution(11216286058925263211)
XLA Ops:
  0.0 267.4 %sums.1 = (bf16[4,896,2304]{2,1,0:T(8,128)(2,1)S(1)}, bf16[4,896,2304]{2,1,0:T(8,128)(2,1)}, bf16[36,2,224,256]{3,2,1,0:T(8,128)(2,1)}, bf16[36,2,112,256]{3,2,1,0:T(8,128)(2,1)}) custom-call(bf16[1,4,4096,896]{3,2,1,0:T(8,128)(2,1)} %a_ref.1, bf16[1,4,4096,2304]{3,2,1,0:T(8,128)(2,1)} %g_ref.1), custom_call_target="tpu_custom_call" | custom-call | tf_op jit(solution)/shard_map/sums/pallas_call | solution.py:392
  267.4 5.9 %write0.1 = (bf16[4,896,2304]{2,1,0:T(8,128)(2,1)}, bf16[8,128]{1,0:T(8,128)(2,1)S(1)}) custom-call(bf16[4,896,2304]{2,1,0:T(8,128)(2,1)S(1)} %get-tuple-element.9.res), custom_call_target="tpu_custom_call" | custom-call | tf_op jit(solution)/shard_map/write0/pallas_call | solution.py:433
  273.3 0.2 later.1.res
  273.5 0.1 write10.1

commit v6 on v5

--- a/solution.py
+++ b/solution.py
@@ -16,7 +16,7 @@
 EVERY, OFFSET = 4, 9
 LATER = 2
 DEEP = 3
-FWD = 3
+FWD = 2
 ACC, V1, V2, SEND = T4 + 1, T4 - T1 + 1, T4 - T3 + 1, 4
 RECV, KEEP = 7, 4
 

time: 277 us -> 277 us (level)
  no operation moved by 1% of the time
where the time goes in v6:
time: 277 us; the launch traced here: 272 us
  Pallas kernels  272 us (98%)
    pallas_call x1, Pallas kernels, local(): pl.pallas_call(functools.partial(sums_kernel, per, pieces), out_shape=(pl...  266 us
    pallas_call x2, Pallas kernels, write(): pl.pallas_call(functools.partial(write_kernel, per, begin, end_even, end_...  6.04 us

profile of v6, /device:TPU:112, one launch (start us, length us, event | category | flops | bytes accessed | tf_op | source)
XLA Modules:
  0.0 272.2 jit_solution(10698558015652293430)
XLA Ops:
  0.0 265.9 %sums.1 = (bf16[4,896,2304]{2,1,0:T(8,128)(2,1)S(1)}, bf16[4,896,2304]{2,1,0:T(8,128)(2,1)}, bf16[36,2,224,256]{3,2,1,0:T(8,128)(2,1)}, bf16[36,2,112,256]{3,2,1,0:T(8,128)(2,1)}) custom-call(bf16[1,4,4096,896]{3,2,1,0:T(8,128)(2,1)} %a_ref.1, bf16[1,4,4096,2304]{3,2,1,0:T(8,128)(2,1)} %g_ref.1), custom_call_target="tpu_custom_call" | custom-call | tf_op jit(solution)/shard_map/sums/pallas_call | solution.py:392
  265.9 5.9 %write0.1 = (bf16[4,896,2304]{2,1,0:T(8,128)(2,1)}, bf16[8,128]{1,0:T(8,128)(2,1)S(1)}) custom-call(bf16[4,896,2304]{2,1,0:T(8,128)(2,1)S(1)} %get-tuple-element.9.res), custom_call_target="tpu_custom_call" | custom-call | tf_op jit(solution)/shard_map/write0/pallas_call | solution.py:433
  271.8 0.2 later.1.res
  272.0 0.1 write10.1

commit v7 on v6

--- a/solution.py
+++ b/solution.py
@@ -132,7 +132,7 @@
             keep_far(k, d).start()
 
     for k in range(FIRST):
-        for copy in first(k):
+        for copy in first(k)[::-1]:
             copy.start()
     load_g(1).start()
 

time: 277 us -> 277 us (level)
  no operation moved by 1% of the time
where the time goes in v7:
time: 277 us; the launch traced here: 272 us
  Pallas kernels  272 us (98%)
    pallas_call x1, Pallas kernels, local(): pl.pallas_call(functools.partial(sums_kernel, per, pieces), out_shape=(pl...  266 us
    pallas_call x2, Pallas kernels, write(): pl.pallas_call(functools.partial(write_kernel, per, begin, end_even, end_...  6.04 us

profile of v7, /device:TPU:112, one launch (start us, length us, event | category | flops | bytes accessed | tf_op | source)
XLA Modules:
  0.0 272.0 jit_solution(3165734542715862407)
XLA Ops:
  0.0 265.8 %sums.1 = (bf16[4,896,2304]{2,1,0:T(8,128)(2,1)S(1)}, bf16[4,896,2304]{2,1,0:T(8,128)(2,1)}, bf16[36,2,224,256]{3,2,1,0:T(8,128)(2,1)}, bf16[36,2,112,256]{3,2,1,0:T(8,128)(2,1)}) custom-call(bf16[1,4,4096,896]{3,2,1,0:T(8,128)(2,1)} %a_ref.1, bf16[1,4,4096,2304]{3,2,1,0:T(8,128)(2,1)} %g_ref.1), custom_call_target="tpu_custom_call" | custom-call | tf_op jit(solution)/shard_map/sums/pallas_call | solution.py:392
  265.8 5.9 %write0.1 = (bf16[4,896,2304]{2,1,0:T(8,128)(2,1)}, bf16[8,128]{1,0:T(8,128)(2,1)S(1)}) custom-call(bf16[4,896,2304]{2,1,0:T(8,128)(2,1)S(1)} %get-tuple-element.9.res), custom_call_target="tpu_custom_call" | custom-call | tf_op jit(solution)/shard_map/write0/pallas_call | solution.py:433
  271.7 0.2 later.1.res
  271.9 0.1 write10.1

commit v8 on v7

--- a/solution.py
+++ b/solution.py
@@ -303,7 +303,7 @@
         forward(final, d, res).wait_recv()
 
 
-def later_kernel(per, groups, res, after, land, sg, rg, sf, rf, sl):
+def later_kernel(per, groups, res, after, land, sg, rg, sf, rf):
     n = 4
     odd = lax.rem(lax.axis_index("rep"), 2)
     me = lax.axis_index("dp")
@@ -330,9 +330,6 @@
     def forward(k, d):
         b = land.at[k, rows_of((left, right)[d], d, half)]
         return remote(b, b, sf.at[k, d], rf.at[k, d], d)
-
-    def keep(k):
-        return pltpu.make_async_copy(own(k), land.at[k, rows_of(me)], sl.at[k])
 
     @pl.when(odd == 1)
     def _():
@@ -343,13 +340,9 @@
         every = [(k, d) for k in range(LATER) for d in range(2)]
         for k, d in every:
             gather(k, d).start()
-        for k in range(LATER):
-            keep(k).start()
         for k, d in every:
             gather(k, d).wait_recv()
             forward(k, d).start()
-        for k in range(LATER):
-            keep(k).wait()
         for k, d in every:
             gather(k, d).wait_send()
             forward(k, d).wait()
@@ -362,19 +355,28 @@
 
     def copy(k):
         p = k * GROUP
-        to = o_ref.at[p // per, :, pl.ds(p % per * WIDTH, GROUP * WIDTH)]
-        part = res.at[k - begin] if begin else res.at[p // per, :, pl.ds(p % per * WIDTH, GROUP * WIDTH)]
-        return pltpu.make_async_copy(part, to, sem.at[k])
+        cols = pl.ds(p % per * WIDTH, GROUP * WIDTH)
+        if not begin:
+            return [pltpu.make_async_copy(res.at[p // per, :, cols], o_ref.at[p // per, :, cols], sem.at[k, 0])]
+        step = o_ref.shape[1] // 4
+        me = lax.axis_index("dp")
+        return [
+            pltpu.make_async_copy(res.at[k - begin, rows], o_ref.at[p // per, rows, cols], sem.at[k, j])
+            for j in range(3)
+            for rows in [pl.ds(pl.multiple_of(lax.rem(me + 1 + j, 4) * step, 16), step)]
+        ]
 
     for k in range(begin, max(end_even, end_odd)):
         @pl.when(k < end)
         def _():
-            copy(k).start()
+            for one in copy(k):
+                one.start()
 
     for k in range(begin, max(end_even, end_odd)):
         @pl.when(k < end)
         def _():
-            copy(k).wait()
+            for one in copy(k):
+                one.wait()
 
 
 def solution(mesh):
@@ -436,19 +438,19 @@
                 in_specs=[vmem, hbm][: len(args)],
                 out_specs=(hbm, hbm),
                 input_output_aliases={1: 0} if begin else {},
-                scratch_shapes=[dma((groups,))],
+                scratch_shapes=[dma((groups, 3))],
                 compiler_params=pltpu.CompilerParams(vmem_limit_bytes=4 * 1024 * 1024),
                 name=f"write{begin}",
             )(*args)
 
         split = groups - LATER
-        out, done = write(0, groups, split, res)
+        out, done = write(0, groups, groups, res)
         later = pl.pallas_call(
             functools.partial(later_kernel, per, groups),
             out_shape=pltpu.VMEM((LATER, d, GROUP * WIDTH), BF16),
             in_specs=[vmem, hbm],
             out_specs=vmem,
-            scratch_shapes=[dma((LATER, 2))] * 4 + [dma((LATER,))],
+            scratch_shapes=[dma((LATER, 2))] * 4,
             compiler_params=pltpu.CompilerParams(
                 collective_id=1, has_side_effects=True, vmem_limit_bytes=4 * 1024 * 1024
             ),

time: 277 us -> 277 us (level)
  no operation moved by 1% of the time
where the time goes in v8:
time: 277 us; the launch traced here: 271 us
  Pallas kernels  271 us (98%)
    pallas_call x1, Pallas kernels, local(): pl.pallas_call(functools.partial(sums_kernel, per, pieces), out_shape=(pl...  265 us
    pallas_call x2, Pallas kernels, write(): pl.pallas_call(functools.partial(write_kernel, per, begin, end_even, end_...  6.49 us

profile of v8, /device:TPU:112, one launch (start us, length us, event | category | flops | bytes accessed | tf_op | source)
XLA Modules:
  0.0 271.4 jit_solution(11069955819955175268)
XLA Ops:
  0.0 264.8 %sums.1 = (bf16[4,896,2304]{2,1,0:T(8,128)(2,1)S(1)}, bf16[4,896,2304]{2,1,0:T(8,128)(2,1)}, bf16[36,2,224,256]{3,2,1,0:T(8,128)(2,1)}, bf16[36,2,112,256]{3,2,1,0:T(8,128)(2,1)}) custom-call(bf16[1,4,4096,896]{3,2,1,0:T(8,128)(2,1)} %a_ref.1, bf16[1,4,4096,2304]{3,2,1,0:T(8,128)(2,1)} %g_ref.1), custom_call_target="tpu_custom_call" | custom-call | tf_op jit(solution)/shard_map/sums/pallas_call | solution.py:394
  264.8 6.1 %write0.1 = (bf16[4,896,2304]{2,1,0:T(8,128)(2,1)}, bf16[8,128]{1,0:T(8,128)(2,1)S(1)}) custom-call(bf16[4,896,2304]{2,1,0:T(8,128)(2,1)S(1)} %get-tuple-element.9.res), custom_call_target="tpu_custom_call" | custom-call | tf_op jit(solution)/shard_map/write0/pallas_call | solution.py:435
  270.9 0.2 later.1.res
  271.1 0.4 write10.1
